TPU v7x, 512 devices: a whole 4x4x16 slice. The times are simulated.
512 devices in a mesh: dp: 32 (over z, core), tp: 16 (over x, y).
Axes of the slice: x: 4, y: 4, z: 16, core: 2. Of those that a mesh axis runs over, the one named last changes fastest.
Arguments:
- partials: bfloat16 [16, 5120, 7680], P('tp', 'dp'), may hold values from -1.5 to 1.5
- layer_input: bfloat16 [7680, 1280], P(('dp', 'tp')), may hold values from -6 to 6
- ln_gain: float32 [1280], replicated, may hold values from 0.25 to 1.75
- ln_bias: float32 [1280], replicated, may hold values from -3 to 3
- fc1_weight: bfloat16 [1280, 5120], P(None, 'tp'), may hold values from -0.15625 to 0.15625
- fc1_bias: float32 [5120], P('tp'), may hold values from -3 to 3
- fc2_weight: bfloat16 [1280, 5120], P(None, 'tp'), may hold values from -0.078125 to 0.078125
- row_rank: int32 [5120, 1], P('dp'), may hold values from 0 to 15; in each aligned block of 160 rows (0 to 159, 160 to 319, ...) at most 15 rows name the same one
Outputs:
- early_grads: bfloat16 [7680, 6400], P(('dp', 'tp'))
- fc1_grad: bfloat16 [1280, 5120], P('dp', 'tp')
- fc2_grad: bfloat16 [1280, 5120], P('dp', 'tp')
Inputs may be any that keep to these rules, and one draw needn't show every extreme that they name: `row_rank`: in each aligned block of 160 rows (one data replica) no rank is named by more than 15 rows, a bound that some block reaches.
All inputs are finite; a program needn't handle non-finite values.
Results may differ from a plain program's by a relative error of at most 0.029.
Values may be sent and summed in bfloat16 or wider, within the bound.
No kernel may reach another device: no remote copies, remote signals or barrier semaphores. Data moves between devices by JAX's collectives and lax.ppermute only.
A program may use at most 64 MiB of HBM per device.

v0:
```python
import jax
import jax.numpy as jnp
from jax import lax
from jax.sharding import PartitionSpec as P


def over_pieces(shard, axis):
    return lax.all_gather(shard, axis).astype(jnp.float32).sum(0)


def joined_along(tiles, dim):
    tiles = jnp.moveaxis(tiles, 0, dim)
    shape = tiles.shape
    return tiles.reshape(*shape[:dim], shape[dim] * shape[dim + 1], *shape[dim + 2 :])


def sent_to_all(shard, axis):
    copies = jnp.broadcast_to(shard, (lax.axis_size(axis), *shard.shape))
    return lax.all_to_all(copies, axis, split_axis=0, concat_axis=0, tiled=True)


def gather_directly(shard, axis, dim):
    return joined_along(sent_to_all(shard, axis), dim)


def cut_along(shard, dim, size):
    before, after = (shard.shape[:dim], shard.shape[dim + 1 :])
    return jnp.moveaxis(shard.reshape(*before, size, -1, *after), dim, 0)


def summed_on_arrival(shard, axis, dim):
    tiles = cut_along(shard, dim, lax.axis_size(axis))
    arrived = lax.all_to_all(tiles, axis, split_axis=0, concat_axis=0, tiled=True)
    return arrived.astype(jnp.float32).sum(axis=0)


def in_one_piece(arrays, axis, dim, along):
    ends, at = ([], 0)
    for a in arrays[:-1]:
        at += a.shape[along]
        ends.append(at)
    both = jnp.concatenate(arrays, axis=along)
    return tuple(jnp.split(summed_on_arrival(both, axis, dim), ends, axis=along))


def gelu_parts(preact):
    normal_cdf = 0.5 * (1.0 + lax.erf(preact * 0.7071067811865476))
    density = jnp.exp(-0.5 * preact * preact) * 0.3989422804014327
    return (preact * normal_cdf, normal_cdf + preact * density)


def slot_matrix(rank_ids, groups, slot_count):
    columns = jnp.arange(groups, dtype=jnp.int32)
    onehot = (rank_ids[:, None] == columns[None, :]).astype(jnp.int32)
    position = jnp.cumsum(onehot, axis=0) - 1
    own_position = jnp.sum(position * onehot, axis=1)
    slot_ids = rank_ids * slot_count + own_position
    targets = jnp.arange(groups * slot_count, dtype=jnp.int32)
    return (targets[:, None] == slot_ids[None, :]).astype(jnp.bfloat16)


def normalize(layer_rows, ln_gain, ln_bias):
    values = layer_rows.astype(jnp.float32)
    row_mean = jnp.mean(values, axis=1, keepdims=True)
    centered = values - row_mean
    row_var = jnp.mean(centered * centered, axis=1, keepdims=True)
    return (centered / jnp.sqrt(row_var + 1e-05) * ln_gain + ln_bias).astype(jnp.bfloat16)


def shards(partials, layer_input, ln_gain, ln_bias, fc1_weight, fc1_bias, fc2_weight, row_rank):
    groups = lax.axis_size("tp")
    replicas = lax.axis_size("dp")
    local_part = partials[0]
    row_count = local_part.shape[0]
    slot_count = layer_input.shape[0]
    feature_width = layer_input.shape[1]
    rank_ids = row_rank[:, 0]
    table = slot_matrix(rank_ids, groups, slot_count)
    normed = normalize(layer_input, ln_gain, ln_bias)
    final_rows = (
        over_pieces(local_part[:, :feature_width].astype(jnp.float32).astype(jnp.bfloat16), "tp")
        .astype(jnp.float32)
        .astype(jnp.bfloat16)
    )
    normed_all = gather_directly(normed, "tp", 0)
    upstream = jnp.dot(table, final_rows, preferred_element_type=jnp.float32).astype(jnp.bfloat16)
    routed_part = local_part[:, feature_width:]
    outgoing = jnp.dot(table, routed_part, preferred_element_type=jnp.float32).astype(jnp.bfloat16)
    outgoing = outgoing.reshape(groups, slot_count, routed_part.shape[1])
    incoming = lax.all_to_all(outgoing, "tp", split_axis=0, concat_axis=0, tiled=True)
    placed = jnp.sum(incoming.astype(jnp.float32), axis=0).astype(jnp.bfloat16)
    preact = jnp.dot(normed_all, fc1_weight, preferred_element_type=jnp.float32) + fc1_bias
    activated, derivative = gelu_parts(preact)
    hidden = activated.astype(jnp.bfloat16)
    hidden_grad = jnp.dot(upstream, fc2_weight, preferred_element_type=jnp.float32)
    preact_grad = (hidden_grad * derivative).astype(jnp.bfloat16)
    factor = float(replicas * row_count) ** (-0.5)
    grad_first = jnp.dot(normed_all.T, preact_grad, preferred_element_type=jnp.float32) * factor
    grad_second = jnp.dot(upstream.T, hidden, preferred_element_type=jnp.float32) * factor
    reduced = in_one_piece(
        (grad_first.astype(jnp.bfloat16), grad_second.astype(jnp.bfloat16)), "dp", 0, 1
    )
    return (placed, reduced[0].astype(jnp.bfloat16), reduced[1].astype(jnp.bfloat16))


def solution(mesh):
    return jax.shard_map(
        shards,
        mesh=mesh,
        in_specs=(
            P("tp", "dp", None),
            P(("dp", "tp"), None),
            P(),
            P(),
            P(None, "tp"),
            P("tp"),
            P(None, "tp"),
            P("dp", None),
        ),
        out_specs=(P(("dp", "tp"), None), P("dp", "tp"), P("dp", "tp")),
        check_vma=False,
    )
```

profile of v0, /device:TPU:1, one launch (start us, length us, event | category | flops | bytes accessed | tf_op | source)
XLA Modules:
  0.0 233.6 jit_solution(7977053167452301517)
XLA Ops:
  7.2 0.0 copy-start
  7.2 0.0 copy-start.1
  7.2 0.0 all-gather.3.cloned.1.call-start
  7.2 1.9 slice.23
  9.1 0.0 all-gather.3.cloned.1.call-update
  9.1 0.9 convert_reduce_fusion
  10.0 1.0 fusion.15
  11.0 0.9 fusion.18
  11.9 0.9 broadcast_in_dim.2
  12.8 7.6 %all-to-all-start.1 = ((bf16[16,15,1280]{2,1,0:T(8,128)(2,1)}), bf16[16,15,1280]{2,1,0:T(8,128)(2,1)S(1)}, u32[]{:S(2)}, u32[]{:S(2)}) async-start(bf16[16,15,1280]{2,1,0:T(8,128)(2,1)} %broadcast_in_dim.2), calls=%async_computation.1 | async-start | bytes 1310720 | tf_op jit(solution)/shard_map/all_to_all | solution.py:19
  20.4 0.6 reduce-window.6
  21.0 0.2 slice_reduce_fusion
  21.2 0.1 bitcast_bitcast_fusion
  21.4 4.3 %convolution_convert_fusion = bf16[240,6400]{1,0:T(8,128)(2,1)} fusion(bf16[160,7680]{1,0:T(8,128)(2,1)} %bitcast.25, s32[160]{0:T(256)S(1)} %multiply_add_fusion), kind=kOutput, calls=%fused_computation | convolution fusion | flops 493094400 | bytes 5120640 | tf_op jit(solution)/shard_map/dot_general | solution.py:88
  25.7 3.6 %reshape.51 = bf16[16,15,6400]{2,1,0:T(8,128)(2,1)} reshape(bf16[240,6400]{1,0:T(8,128)(2,1)} %convolution_convert_fusion) | data formatting | bytes 6144000 | tf_op jit(solution)/shard_map/reshape | solution.py:89
  29.3 1.5 all-to-all-done.1
  30.8 5.4 %all-to-all-start = ((bf16[16,15,6400]{2,1,0:T(8,128)(2,1)}), bf16[16,15,6400]{2,1,0:T(8,128)(2,1)}, u32[]{:S(2)}, u32[]{:S(2)}) async-start(bf16[16,15,6400]{2,1,0:T(8,128)(2,1)} %reshape.51), calls=%async_computation | async-start | bytes 6553600 | tf_op jit(solution)/shard_map/all_to_all | solution.py:90
  36.1 0.2 reshape.52
  36.3 1.5 convolution_add_fusion
  37.9 84.4 %all-gather.3.cloned.1.call-done = bf16[2560,1280]{1,0:T(8,128)(2,1)} async-done(((bf16[160,1280]{1,0:T(8,128)(2,1)}), bf16[2560,1280]{1,0:T(8,128)(2,1)}) %all-gather.3.cloned.1.call-update) | async-done | bytes 6553616 | tf_op jit(solution)/shard_map/all_gather | solution.py:8
  122.3 3.9 %reduce_sum.64 = bf16[160,1280]{1,0:T(8,128)(2,1)S(1)} reduce(bf16[16,160,1280]{2,1,0:T(8,128)(2,1)} %bitcast.23, bf16[]{:T(256)} %constant.26.clone.1), dimensions={0}, to_apply=%region_6.7 | reduce | flops 3072000 | bytes 6963202 | tf_op jit(solution)/shard_map/reduce_sum | solution.py:8
  126.2 0.3 convolution_convert_fusion.1
  126.5 0.4 fusion.1
  126.9 2.0 fusion
  128.9 1.2 pad_maximum_fusion
  130.1 2.2 copy.13
  132.3 0.0 all-to-all-done
  132.3 13.2 %all-to-all-start.2 = ((bf16[32,40,640]{2,1,0:T(8,128)(2,1)}), bf16[32,40,640]{2,1,0:T(8,128)(2,1)S(1)}, u32[]{:S(2)}, u32[]{:S(2)}) async-start(bf16[32,40,640]{2,1,0:T(8,128)(2,1)} %bitcast.4), calls=%async_computation.2 | async-start | bytes 3276800 | tf_op jit(solution)/shard_map/all_to_all | solution.py:33
  145.5 3.2 %reduce_sum.61 = bf16[15,6400]{1,0:T(8,128)(2,1)} reduce(bf16[16,15,6400]{2,1,0:T(8,128)(2,1)} %all-to-all-done, bf16[]{:T(256)} %constant.26.clone.1), dimensions={0}, to_apply=%region_3.4 | reduce | flops 1440000 | bytes 3264002 | tf_op jit(solution)/shard_map/reduce_sum | solution.py:91
  148.7 77.1 %all-to-all-done.2 = bf16[32,40,640]{2,1,0:T(8,128)(2,1)S(1)} async-done(((bf16[32,40,640]{2,1,0:T(8,128)(2,1)}), bf16[32,40,640]{2,1,0:T(8,128)(2,1)S(1)}, u32[]{:S(2)}, u32[]{:S(2)}) %all-to-all-start.2) | async-done | bytes 1638432 | tf_op jit(solution)/shard_map/all_to_all | solution.py:33
  225.8 0.2 reduce.2
  226.0 0.7 fusion.23
  (12 shorter events, 0.1 us)
Async XLA Ops:
  7.2 119.7 %copy-start = (bf16[1280,320]{0,1:T(8,128)(2,1)S(1)}, bf16[1280,320]{0,1:T(8,128)(2,1)}, u32[]{:S(2)}) copy-start(bf16[1280,320]{0,1:T(8,128)(2,1)} %param.14) | copy-start | bytes 2457604
  7.2 13.2 %copy-start.1 = (s32[160,1]{0,1:T(1,128)S(1)}, s32[160,1]{0,1:T(1,128)}, u32[]{:S(2)}) copy-start(s32[160,1]{0,1:T(1,128)} %param.15) | copy-start | bytes 1924
  7.2 115.1 %all-gather.3.cloned.1.call-start = ((), (), s32[]{:S(2)}) async-start(), calls=%async_computation.3 | async-start | bytes 6963200 | tf_op jit(solution)/shard_map/all_gather | solution.py:8
  12.8 18.0 %all-to-all-start.1 = ((bf16[16,15,1280]{2,1,0:T(8,128)(2,1)}), bf16[16,15,1280]{2,1,0:T(8,128)(2,1)S(1)}, u32[]{:S(2)}, u32[]{:S(2)}) async-start(bf16[16,15,1280]{2,1,0:T(8,128)(2,1)} %broadcast_in_dim.2), calls=%async_computation.1 | async-start | bytes 1310720 | tf_op jit(solution)/shard_map/all_to_all | solution.py:19
  29.3 7.1 %copy-start.2 = (f32[320]{0:T(512)S(1)}, f32[320]{0:T(512)}, u32[]{:S(2)}) copy-start(f32[320]{0:T(512)} %param.13) | copy-start | bytes 3844
  30.8 101.6 %all-to-all-start = ((bf16[16,15,6400]{2,1,0:T(8,128)(2,1)}), bf16[16,15,6400]{2,1,0:T(8,128)(2,1)}, u32[]{:S(2)}, u32[]{:S(2)}) async-start(bf16[16,15,6400]{2,1,0:T(8,128)(2,1)} %reshape.51), calls=%async_computation | async-start | bytes 6553600 | tf_op jit(solution)/shard_map/all_to_all | solution.py:90
  132.3 93.5 %all-to-all-start.2 = ((bf16[32,40,640]{2,1,0:T(8,128)(2,1)}), bf16[32,40,640]{2,1,0:T(8,128)(2,1)S(1)}, u32[]{:S(2)}, u32[]{:S(2)}) async-start(bf16[32,40,640]{2,1,0:T(8,128)(2,1)} %bitcast.4), calls=%async_computation.2 | async-start | bytes 3276800 | tf_op jit(solution)/shard_map/all_to_all | solution.py:33
Sparse Core Ops, SparseCore 0:
  11.1 111.1 all-gather.2
where the time goes:
time: 234 us
  waiting for transfers between devices  163 us (70%)
  starting transfers between devices  26.1 us (11%)
  between operations  14.2 us (6%)
  other arithmetic  12.1 us (5%)
  local copies, waits for them, and re-layouts  9.7 us (4%)
  matrix products  8.51 us (4%)
    all_gather x1, waiting for transfers between devices, over_pieces(): return lax.all_gather(shard, axis).astype(jnp.float32).sum(0)  84.4 us
    all_to_all x1, waiting for transfers between devices, summed_on_arrival(): lax.all_to_all(tiles, axis, split_axis=0, concat_axis=0, tiled=True)  77.1 us
    all_to_all x1, starting transfers between devices, summed_on_arrival(): lax.all_to_all(tiles, axis, split_axis=0, concat_axis=0, tiled=True)  13.2 us
    all_to_all x1, starting transfers between devices, sent_to_all(): return lax.all_to_all(copies, axis, split_axis=0, concat_axis=0, tiled=True)  7.57 us
    all_to_all x1, starting transfers between devices, shards(): lax.all_to_all(outgoing, 'tp', split_axis=0, concat_axis=0, tiled=True)  5.35 us
  transfers between devices with their start and end apart: 4, of which 3 were waited for; matrix products, arithmetic and copies ran while one was open for 12% of the time, Pallas kernels for 0%

commit v1 on v0

v1 whole, which is shorter than its diff:
```python
import functools

import jax
import jax.numpy as jnp
from jax import lax
from jax.experimental import pallas as pl
from jax.experimental.pallas import tpu as pltpu
from jax.sharding import PartitionSpec as P

SUB, LANE = 8, 128
SLOT_PAD = 16


def tile_places(rows, width, parts):
    across = width // LANE
    total = (rows // SUB) * across
    whole = total // parts
    places = []
    for t in range(total):
        r, c = divmod(t, across)
        if t < whole * parts:
            places.append((*divmod(t, whole), 0, SUB, r * SUB, c * LANE))
        else:
            half = SUB // 2
            for h in range(2):
                part = 2 * (t - whole * parts) + h
                places.append((part, whole, 0, half, r * SUB + h * half, c * LANE))
    return whole + 1, places


def cut_kernel(places, x_ref, out_ref):
    last = out_ref.shape[1] - 1
    for part in range(out_ref.shape[0]):
        out_ref[part, last] = jnp.zeros(out_ref.shape[2:], out_ref.dtype)
    for part, i, at, size, r, c in places:
        out_ref[part, i, at : at + size, :] = x_ref[r : r + size, c : c + LANE]


def cut_tiles(x, width, parts):
    rows = x.shape[0]
    depth, places = tile_places(rows, width, parts)
    return pl.pallas_call(
        functools.partial(cut_kernel, places),
        grid=(1,),
        in_specs=[pl.BlockSpec((rows, width), lambda i: (0, 0))],
        out_specs=pl.BlockSpec((parts, depth, SUB, LANE), lambda i: (0, 0, 0, 0)),
        out_shape=jax.ShapeDtypeStruct((parts, depth, SUB, LANE), x.dtype),
        name="cut_tiles",
    )(x)


def grads_kernel(places, factor, tiles_ref, table_ref, normed_ref, hidden_ref, deriv_ref, weight_ref, out_ref, rows_ref, up_ref, pg_ref):
    for part, i, at, size, r, c in places:
        rows_ref[r : r + size, c : c + LANE] = tiles_ref[part, i, at : at + size, :]
    up_ref[...] = jnp.dot(table_ref[...], rows_ref[...], preferred_element_type=jnp.float32).astype(jnp.bfloat16)
    hidden_grad = lax.dot_general(
        up_ref[...], weight_ref[...], (((1,), (1,)), ((), ())), preferred_element_type=jnp.float32
    )
    units = hidden_grad.shape[1]
    pg_ref[...] = jnp.zeros_like(pg_ref)
    pg_ref[:, :units] = (hidden_grad * deriv_ref[...]).astype(jnp.bfloat16)
    cores, near, far, block, _ = out_ref.shape
    wide = pg_ref.shape[1]
    keep = wide - LANE
    step = 5 * LANE
    for at in range(0, normed_ref.shape[1], step):
        dims = (((0,), (0,)), ((), ()))
        first = lax.dot_general(normed_ref[:, at : at + step], pg_ref[...], dims, preferred_element_type=jnp.float32)
        second = lax.dot_general(up_ref[:, at : at + step], hidden_ref[...], dims, preferred_element_type=jnp.float32)
        for b in range(0, step, block):
            k = (at + b) // block
            z, core = divmod(k, cores)
            m, p = divmod(z, near)
            one, two = first[b : b + block] * factor, second[b : b + block] * factor
            out_ref[core, p, m, :, :keep] = one[:, :keep].astype(jnp.bfloat16)
            out_ref[core, p, m, :, keep:wide] = (one[:, keep:] + two[:, :LANE]).astype(jnp.bfloat16)
            out_ref[core, p, m, :, wide:] = two[:, LANE:].astype(jnp.bfloat16)


def grad_terms(tiles, table, normed, hidden, deriv, weight_t, factor, shape):
    slots, width = normed.shape
    rows = table.shape[1]
    _, places = tile_places(rows, width, tiles.shape[0])
    return pl.pallas_call(
        functools.partial(grads_kernel, places, factor),
        out_shape=jax.ShapeDtypeStruct(shape, jnp.bfloat16),
        scratch_shapes=[
            pltpu.VMEM((rows, width), jnp.bfloat16),
            pltpu.VMEM((slots, width), jnp.bfloat16),
            pltpu.VMEM((slots, hidden.shape[1]), jnp.bfloat16),
        ],
        name="grad_terms",
    )(tiles, table, normed, hidden, deriv, weight_t)


def exchange(blocks, axis, groups=None):
    return lax.all_to_all(blocks, axis, 0, 0, tiled=True, axis_index_groups=groups)


def to_all(shard, axis):
    return exchange(jnp.broadcast_to(shard, (lax.axis_size(axis), *shard.shape)), axis)


def total(arrived):
    return arrived.astype(jnp.float32).sum(axis=0).astype(jnp.bfloat16)


def gelu_parts(preact):
    normal_cdf = 0.5 * (1.0 + lax.erf(preact * 0.7071067811865476))
    density = jnp.exp(-0.5 * preact * preact) * 0.3989422804014327
    return (preact * normal_cdf, normal_cdf + preact * density)


def slot_matrix(rank_ids, groups):
    columns = jnp.arange(groups, dtype=jnp.int32)
    onehot = (rank_ids[:, None] == columns[None, :]).astype(jnp.int32)
    position = jnp.cumsum(onehot, axis=0) - 1
    own_position = jnp.sum(position * onehot, axis=1)
    slot_ids = rank_ids * SLOT_PAD + own_position
    targets = jnp.arange(groups * SLOT_PAD, dtype=jnp.int32)
    return (targets[:, None] == slot_ids[None, :]).astype(jnp.bfloat16)


def normalize(layer_rows, ln_gain, ln_bias):
    values = layer_rows.astype(jnp.float32)
    row_mean = jnp.mean(values, axis=1, keepdims=True)
    centered = values - row_mean
    row_var = jnp.mean(centered * centered, axis=1, keepdims=True)
    return (centered / jnp.sqrt(row_var + 1e-05) * ln_gain + ln_bias).astype(jnp.bfloat16)


def dp_groups(replicas):
    cores, near = 2, 4
    depth = replicas // cores
    far = depth // near
    pairs = [[cores * z + c for c in range(cores)] for z in range(depth)]
    close = []
    for g in range(far):
        close.append([cores * (near * g + p) for p in range(near)])
    for g in range(far):
        zs = [(near * (g + 1) + p) % depth if p < near // 2 else near * g + p for p in range(near)]
        close.append([cores * z + 1 for z in zs])
    strided = [[cores * (near * m + p) + c for m in range(far)] for p in range(near) for c in range(cores)]
    return cores, near, far, pairs, close, strided


def shards(partials, layer_input, ln_gain, ln_bias, fc1_weight, fc1_bias, fc2_weight, row_rank):
    groups = lax.axis_size("tp")
    replicas = lax.axis_size("dp")
    local_part = partials[0]
    row_count = local_part.shape[0]
    slot_count, width = layer_input.shape
    units = fc1_weight.shape[1]
    cores, near, far, pairs, close, strided = dp_groups(replicas)
    block = width // replicas

    outgoing = cut_tiles(local_part, width, groups)
    own_tiles = total(exchange(outgoing, "tp"))
    tiles = to_all(own_tiles, "tp")

    table = slot_matrix(row_rank[:, 0], groups)
    normed = normalize(layer_input, ln_gain, ln_bias)
    normed = jnp.pad(normed, ((0, SLOT_PAD - slot_count), (0, 0)))
    normed_all = to_all(normed, "tp").reshape(groups * SLOT_PAD, width)
    preact = jnp.dot(normed_all, fc1_weight, preferred_element_type=jnp.float32) + fc1_bias
    activated, derivative = gelu_parts(preact)
    hidden = jnp.pad(activated.astype(jnp.bfloat16), ((0, 0), (-units % LANE, 0)))

    routed = jnp.dot(table, local_part[:, width:], preferred_element_type=jnp.float32).astype(jnp.bfloat16)
    incoming = exchange(routed.reshape(groups, SLOT_PAD, routed.shape[1]), "tp")

    factor = float(replicas * row_count) ** (-0.5)
    terms = grad_terms(
        tiles, table, normed_all, hidden, derivative, fc2_weight.T, factor,
        (cores, near, far, block, 2 * units),
    )
    both = total(exchange(terms, "dp", pairs))
    both = total(exchange(both, "dp", close))
    both = total(exchange(both, "dp", strided))
    placed = total(incoming)[:slot_count]
    return (placed, both[:, :units], both[:, units:])


def solution(mesh):
    return jax.shard_map(
        shards,
        mesh=mesh,
        in_specs=(
            P("tp", "dp", None),
            P(("dp", "tp"), None),
            P(),
            P(),
            P(None, "tp"),
            P("tp"),
            P(None, "tp"),
            P("dp", None),
        ),
        out_specs=(P(("dp", "tp"), None), P("dp", "tp"), P("dp", "tp")),
        check_vma=False,
    )
```

time: 234 us -> 170 us (0.73)
  waiting for transfers between devices: 163 us -> 79.7 us
  starting transfers between devices: 26.1 us -> 48.4 us
  blocking collectives: 0 us -> 13.8 us
  between operations: 14.2 us -> 0.79 us
  Pallas kernels: 0 us -> 6.35 us
  local copies, waits for them, and re-layouts: 9.7 us -> 4.22 us
  matrix products: 8.51 us -> 4.05 us
    all_gather x1 -> x0, waiting for transfers between devices: 84.4 us -> none  [over_pieces(): return lax.all_gather(shard, axis).astype(jnp.float32).sum(0)]
    all_to_all x3 -> x6, starting transfers between devices: 26.1 us -> 48.4 us  [exchange(): lax.all_to_all(blocks, axis, 0, 0, tiled=True, axis_index_groups=groups)]
    all_to_all x0 -> x1, blocking collectives: none -> 13.8 us  [exchange(): lax.all_to_all(blocks, axis, 0, 0, tiled=True, axis_index_groups=groups)]
    pallas_call x0 -> x2, Pallas kernels: none -> 6.35 us  [the longest x1 4.5 us: grad_terms(): pl.pallas_call(functools.partial(grads_kernel, places, factor), out_shape...]
    dot_general x4 -> x1, matrix products: 6.96 us -> 2.69 us  [shards(): jnp.dot(table, local_part[:, width:], preferred_element_type=jnp.float32)]
    reshape x2 -> x0, local copies, waits for them, and re-layouts: 3.83 us -> none  [the longest x1 3.63 us: shards(): outgoing = outgoing.reshape(groups, slot_count, routed_part.shape[1])]
    all_to_all x3 -> x6, waiting for transfers between devices: 78.6 us -> 79.7 us  [exchange(): lax.all_to_all(blocks, axis, 0, 0, tiled=True, axis_index_groups=groups)]
    reduce_sum x3 -> x5, other arithmetic: 7.35 us -> 8.16 us  [total(): return arrived.astype(jnp.float32).sum(axis=0).astype(jnp.bfloat16)]
  transfers between devices with their start and end apart: 4 -> 6, of which waited for: 3 -> 6; matrix products, arithmetic and copies ran while one was open for 12% -> 7% of each run, Pallas kernels for 0% -> 0%
where the time goes in v1:
time: 170 us; the launch traced here: 167 us
  waiting for transfers between devices  79.7 us (47%)
  starting transfers between devices  48.4 us (28%)
  blocking collectives  13.8 us (8%)
  other arithmetic  10 us (6%)
  Pallas kernels  6.35 us (4%)
  local copies, waits for them, and re-layouts  4.22 us (2%)
  matrix products  4.05 us (2%)
    all_to_all x6, waiting for transfers between devices, exchange(): lax.all_to_all(blocks, axis, 0, 0, tiled=True, axis_index_groups=groups)  79.7 us
    all_to_all x6, starting transfers between devices, exchange(): lax.all_to_all(blocks, axis, 0, 0, tiled=True, axis_index_groups=groups)  48.4 us
    all_to_all x1, blocking collectives, exchange(): lax.all_to_all(blocks, axis, 0, 0, tiled=True, axis_index_groups=groups)  13.8 us
    reduce_sum x5, other arithmetic, total(): return arrived.astype(jnp.float32).sum(axis=0).astype(jnp.bfloat16)  8.16 us
    pallas_call x1, Pallas kernels, grad_terms(): pl.pallas_call(functools.partial(grads_kernel, places, factor), out_shape...  4.5 us
  transfers between devices with their start and end apart: 6, of which 6 were waited for; matrix products, arithmetic and copies ran while one was open for 7% of the time, Pallas kernels for 0%

profile of v1, /device:TPU:1, one launch (start us, length us, event | category | flops | bytes accessed | tf_op | source)
XLA Modules:
  0.0 167.3 jit_solution(14158745451248576961)
XLA Ops:
  0.7 1.9 %cut_tiles.1 = bf16[16,13,8,128]{3,2,1,0:T(8,128)(2,1)} custom-call(bf16[160,7680]{1,0:T(8,128)(2,1)} %bitcast.21), custom_call_target="tpu_custom_call" | custom-call | tf_op jit(solution)/shard_map/cut_tiles/pallas_call | solution.py:42
  2.5 7.7 %all-to-all-start.1 = ((bf16[16,13,8,128]{3,2,1,0:T(8,128)(2,1)}), bf16[16,13,8,128]{3,2,1,0:T(8,128)(2,1)S(1)}, u32[]{:S(2)}, u32[]{:S(2)}) async-start(bf16[16,13,8,128]{3,2,1,0:T(8,128)(2,1)} %cut_tiles.1), calls=%async_computation.1 | async-start | bytes 851968 | tf_op jit(solution)/shard_map/all_to_all | solution.py:97
  10.3 0.1 convert_reduce_fusion
  10.4 0.2 fusion.9
  10.6 0.6 reduce-window.6
  11.2 0.1 fusion.12
  11.3 7.1 %all-to-all-done.1 = bf16[16,13,8,128]{3,2,1,0:T(8,128)(2,1)S(1)} async-done(((bf16[16,13,8,128]{3,2,1,0:T(8,128)(2,1)}), bf16[16,13,8,128]{3,2,1,0:T(8,128)(2,1)S(1)}, u32[]{:S(2)}, u32[]{:S(2)}) %all-to-all-start.1) | async-done | bytes 426016 | tf_op jit(solution)/shard_map/all_to_all | solution.py:97
  18.4 0.9 broadcast_in_dim.5
  19.3 3.7 %all-to-all-start.3 = ((bf16[16,16,1280]{2,1,0:T(8,128)(2,1)}), bf16[16,16,1280]{2,1,0:T(8,128)(2,1)S(1)}, u32[]{:S(2)}, u32[]{:S(2)}) async-start(bf16[16,16,1280]{2,1,0:T(8,128)(2,1)} %broadcast_in_dim.5), calls=%async_computation.3 | async-start | bytes 1310720 | tf_op jit(solution)/shard_map/all_to_all | solution.py:97
  23.0 0.2 slice_reduce_fusion
  23.3 0.1 bitcast_bitcast_fusion
  23.4 9.3 %all-to-all-done.3 = bf16[16,16,1280]{2,1,0:T(8,128)(2,1)S(1)} async-done(((bf16[16,16,1280]{2,1,0:T(8,128)(2,1)}), bf16[16,16,1280]{2,1,0:T(8,128)(2,1)S(1)}, u32[]{:S(2)}, u32[]{:S(2)}) %all-to-all-start.3) | async-done | bytes 655392 | tf_op jit(solution)/shard_map/all_to_all | solution.py:97
  32.8 0.9 broadcast_in_dim.4
  33.6 3.6 %all-to-all-start.2 = ((bf16[16,13,8,128]{3,2,1,0:T(8,128)(2,1)}), bf16[16,13,8,128]{3,2,1,0:T(8,128)(2,1)S(1)}, u32[]{:S(2)}, u32[]{:S(2)}) async-start(bf16[16,13,8,128]{3,2,1,0:T(8,128)(2,1)} %broadcast_in_dim.4), calls=%async_computation.2 | async-start | bytes 851968 | tf_op jit(solution)/shard_map/all_to_all | solution.py:97
  37.2 0.7 fusion.5.table_ref
  37.9 1.4 fusion.4
  39.2 0.8 pad.14.hidden_ref
  40.0 5.5 %all-to-all-done.2.tiles_ref = bf16[16,13,8,128]{3,2,1,0:T(8,128)(2,1)S(1)} async-done(((bf16[16,13,8,128]{3,2,1,0:T(8,128)(2,1)}), bf16[16,13,8,128]{3,2,1,0:T(8,128)(2,1)S(1)}, u32[]{:S(2)}, u32[]{:S(2)}) %all-to-all-start.2) | async-done | bytes 426016 | tf_op jit(solution)/shard_map/all_to_all | solution.py:97
  45.6 0.8 copy-done.3
  46.3 4.5 %grad_terms.1 = bf16[2,4,4,40,640]{4,3,2,1,0:T(8,128)(2,1)} custom-call(bf16[16,13,8,128]{3,2,1,0:T(8,128)(2,1)} %copy-done.3, bf16[256,160]{1,0:T(8,128)(2,1)} %fusion.5.table_ref, bf16[256,1280]{1,0:T(8,128)(2,1)} %bitcast.24, bf16[256,384]{1,0:T(8,128)(2,1)} %pad.14.hidden_ref, f32[256,320]{1,0:T(8,128)} %get-tuple-element.3.deriv_ref, ...), custom_call_target="tpu_custom_call" | custom-call | tf_op jit(solution)/shard_map/grad_terms/pallas_call | solution.py:84
  50.8 13.8 %all_to_all.35 = bf16[2,4,4,40,640]{4,3,2,1,0:T(8,128)(2,1)} all-to-all(bf16[2,4,4,40,640]{4,3,2,1,0:T(8,128)(2,1)} %grad_terms.1), channel_id=1, replica_groups={{0,16},{32,48},{64,80},{96,112},{128,144},{160,176},{192,208},{224,240}..., dimensions={0} | all-to-all | bytes 3276800 | tf_op jit(solution)/shard_map/all_to_all | solution.py:97
  64.6 3.0 %reduce_sum.92 = bf16[4,4,40,640]{3,2,1,0:T(8,128)(2,1)} reduce(bf16[2,4,4,40,640]{4,3,2,1,0:T(8,128)(2,1)} %all_to_all.35, bf16[]{:T(256)} %constant.29.clone.1), dimensions={0}, to_apply=%region_7.8 | reduce | flops 409600 | bytes 2457602 | tf_op jit(solution)/shard_map/reduce_sum | solution.py:105
  67.6 10.8 %all-to-all-start.5 = ((bf16[4,4,40,640]{3,2,1,0:T(8,128)(2,1)}), bf16[4,4,40,640]{3,2,1,0:T(8,128)(2,1)}, u32[]{:S(2)}, u32[]{:S(2)}) async-start(bf16[4,4,40,640]{3,2,1,0:T(8,128)(2,1)} %reduce_sum.92), calls=%async_computation.5 | async-start | bytes 1638400 | tf_op jit(solution)/shard_map/all_to_all | solution.py:97
  78.4 2.7 %convolution_convert_fusion = bf16[256,6400]{1,0:T(8,128)(2,1)} fusion(bf16[160,7680]{1,0:T(8,128)(2,1)S(1)} %bitcast.22, s32[160]{0:T(256)S(1)} %multiply_add_fusion), kind=kOutput, calls=%fused_computation | convolution fusion | flops 525967360 | bytes 5325824 | tf_op jit(solution)/shard_map/dot_general | solution.py:169
  81.1 15.6 %all-to-all-done.5 = bf16[4,4,40,640]{3,2,1,0:T(8,128)(2,1)} async-done(((bf16[4,4,40,640]{3,2,1,0:T(8,128)(2,1)}), bf16[4,4,40,640]{3,2,1,0:T(8,128)(2,1)}, u32[]{:S(2)}, u32[]{:S(2)}) %all-to-all-start.5) | async-done | bytes 819232 | tf_op jit(solution)/shard_map/all_to_all | solution.py:97
  96.7 4.5 %all-to-all-start = ((bf16[16,16,6400]{2,1,0:T(8,128)(2,1)}), bf16[16,16,6400]{2,1,0:T(8,128)(2,1)}, u32[]{:S(2)}, u32[]{:S(2)}) async-start(bf16[16,16,6400]{2,1,0:T(8,128)(2,1)} %bitcast.20), calls=%async_computation | async-start | bytes 6553600 | tf_op jit(solution)/shard_map/all_to_all | solution.py:97
  101.2 2.0 %reduce_sum.93 = bf16[4,40,640]{2,1,0:T(8,128)(2,1)} reduce(bf16[4,4,40,640]{3,2,1,0:T(8,128)(2,1)} %all-to-all-done.5, bf16[]{:T(256)} %constant.29.clone.1), dimensions={0}, to_apply=%region_8.9 | reduce | flops 307200 | bytes 1024002 | tf_op jit(solution)/shard_map/reduce_sum | solution.py:105
  103.2 28.6 %all-to-all-done = bf16[16,16,6400]{2,1,0:T(8,128)(2,1)} async-done(((bf16[16,16,6400]{2,1,0:T(8,128)(2,1)}), bf16[16,16,6400]{2,1,0:T(8,128)(2,1)}, u32[]{:S(2)}, u32[]{:S(2)}) %all-to-all-start) | async-done | bytes 3276832 | tf_op jit(solution)/shard_map/all_to_all | solution.py:97
  131.8 18.1 %all-to-all-start.6 = ((bf16[4,40,640]{2,1,0:T(8,128)(2,1)}), bf16[4,40,640]{2,1,0:T(8,128)(2,1)S(1)}, u32[]{:S(2)}, u32[]{:S(2)}) async-start(bf16[4,40,640]{2,1,0:T(8,128)(2,1)} %reduce_sum.93), calls=%async_computation.6 | async-start | bytes 409600 | tf_op jit(solution)/shard_map/all_to_all | solution.py:97
  149.9 3.1 %reduce_sum.88 = bf16[16,6400]{1,0:T(8,128)(2,1)} reduce(bf16[16,16,6400]{2,1,0:T(8,128)(2,1)} %all-to-all-done, bf16[]{:T(256)} %constant.29.clone.1), dimensions={0}, to_apply=%region_3.4 | reduce | flops 1536000 | bytes 3481602 | tf_op jit(solution)/shard_map/reduce_sum | solution.py:105
  153.0 13.6 %all-to-all-done.6 = bf16[4,40,640]{2,1,0:T(8,128)(2,1)S(1)} async-done(((bf16[4,40,640]{2,1,0:T(8,128)(2,1)}), bf16[4,40,640]{2,1,0:T(8,128)(2,1)S(1)}, u32[]{:S(2)}, u32[]{:S(2)}) %all-to-all-start.6) | async-done | bytes 204832 | tf_op jit(solution)/shard_map/all_to_all | solution.py:97
  166.6 0.7 fusion.15
  (28 shorter events, 0.3 us)
Async XLA Ops:
  0.6 37.3 %copy-start = (bf16[1280,320]{0,1:T(8,128)(2,1)S(1)}, bf16[1280,320]{0,1:T(8,128)(2,1)}, u32[]{:S(2)}) copy-start(bf16[1280,320]{0,1:T(8,128)(2,1)} %param.12) | copy-start | bytes 2457604
  0.6 9.6 %copy-start.5 = (s32[160,1]{0,1:T(1,128)S(1)}, s32[160,1]{0,1:T(1,128)}, u32[]{:S(2)}) copy-start(s32[160,1]{0,1:T(1,128)} %param.15) | copy-start | bytes 1924
  0.7 9.6 %copy-start.4 = (bf16[15,1280]{1,0:T(8,128)(2,1)S(1)}, bf16[15,1280]{1,0:T(8,128)(2,1)}, u32[]{:S(2)}) copy-start(bf16[15,1280]{1,0:T(8,128)(2,1)} %param.9) | copy-start | bytes 115204
  0.7 10.6 %copy-start.6 = (f32[1280]{0:T(1024)S(1)}, f32[1280]{0:T(1024)}, u32[]{:S(2)}) copy-start(f32[1280]{0:T(1024)} %param.11) | copy-start | bytes 15364
  0.7 10.6 %copy-start.7 = (f32[1280]{0:T(1024)S(1)}, f32[1280]{0:T(1024)}, u32[]{:S(2)}) copy-start(f32[1280]{0:T(1024)} %param.10) | copy-start | bytes 15364
  2.5 35.3 %copy-start.8 = (f32[320]{0:T(512)S(1)}, f32[320]{0:T(512)}, u32[]{:S(2)}) copy-start(f32[320]{0:T(512)} %param.13) | copy-start | bytes 3844
  2.5 15.9 %all-to-all-start.1 = ((bf16[16,13,8,128]{3,2,1,0:T(8,128)(2,1)}), bf16[16,13,8,128]{3,2,1,0:T(8,128)(2,1)S(1)}, u32[]{:S(2)}, u32[]{:S(2)}) async-start(bf16[16,13,8,128]{3,2,1,0:T(8,128)(2,1)} %cut_tiles.1), calls=%async_computation.1 | async-start | bytes 851968 | tf_op jit(solution)/shard_map/all_to_all | solution.py:97
  19.3 13.5 %all-to-all-start.3 = ((bf16[16,16,1280]{2,1,0:T(8,128)(2,1)}), bf16[16,16,1280]{2,1,0:T(8,128)(2,1)S(1)}, u32[]{:S(2)}, u32[]{:S(2)}) async-start(bf16[16,16,1280]{2,1,0:T(8,128)(2,1)} %broadcast_in_dim.5), calls=%async_computation.3 | async-start | bytes 1310720 | tf_op jit(solution)/shard_map/all_to_all | solution.py:97
  32.8 12.8 %copy-start.2 = (bf16[16,16,1280]{2,1,0:T(8,128)(2,1)}, bf16[16,16,1280]{2,1,0:T(8,128)(2,1)S(1)}, u32[]{:S(2)}) copy-start(bf16[16,16,1280]{2,1,0:T(8,128)(2,1)S(1)} %all-to-all-done.3) | copy-start | bytes 1966084
  33.6 11.9 %all-to-all-start.2 = ((bf16[16,13,8,128]{3,2,1,0:T(8,128)(2,1)}), bf16[16,13,8,128]{3,2,1,0:T(8,128)(2,1)S(1)}, u32[]{:S(2)}, u32[]{:S(2)}) async-start(bf16[16,13,8,128]{3,2,1,0:T(8,128)(2,1)} %broadcast_in_dim.4), calls=%async_computation.2 | async-start | bytes 851968 | tf_op jit(solution)/shard_map/all_to_all | solution.py:97
  45.6 0.8 copy-start.3
  64.6 13.8 %copy-start.1 = (bf16[1,160,7680]{2,1,0:T(8,128)(2,1)S(1)}, bf16[1,160,7680]{2,1,0:T(8,128)(2,1)}, u32[]{:S(2)}) copy-start(bf16[1,160,7680]{2,1,0:T(8,128)(2,1)} %param.8) | copy-start | bytes 7372804
  67.6 29.1 %all-to-all-start.5 = ((bf16[4,4,40,640]{3,2,1,0:T(8,128)(2,1)}), bf16[4,4,40,640]{3,2,1,0:T(8,128)(2,1)}, u32[]{:S(2)}, u32[]{:S(2)}) async-start(bf16[4,4,40,640]{3,2,1,0:T(8,128)(2,1)} %reduce_sum.92), calls=%async_computation.5 | async-start | bytes 1638400 | tf_op jit(solution)/shard_map/all_to_all | solution.py:97
  96.7 35.1 %all-to-all-start = ((bf16[16,16,6400]{2,1,0:T(8,128)(2,1)}), bf16[16,16,6400]{2,1,0:T(8,128)(2,1)}, u32[]{:S(2)}, u32[]{:S(2)}) async-start(bf16[16,16,6400]{2,1,0:T(8,128)(2,1)} %bitcast.20), calls=%async_computation | async-start | bytes 6553600 | tf_op jit(solution)/shard_map/all_to_all | solution.py:97
  131.8 34.8 %all-to-all-start.6 = ((bf16[4,40,640]{2,1,0:T(8,128)(2,1)}), bf16[4,40,640]{2,1,0:T(8,128)(2,1)S(1)}, u32[]{:S(2)}, u32[]{:S(2)}) async-start(bf16[4,40,640]{2,1,0:T(8,128)(2,1)} %reduce_sum.93), calls=%async_computation.6 | async-start | bytes 409600 | tf_op jit(solution)/shard_map/all_to_all | solution.py:97

commit v2 on v1

--- a/solution.py
+++ b/solution.py
@@ -28,25 +28,82 @@
     return whole + 1, places
 
 
-def cut_kernel(places, x_ref, out_ref):
-    last = out_ref.shape[1] - 1
-    for part in range(out_ref.shape[0]):
-        out_ref[part, last] = jnp.zeros(out_ref.shape[2:], out_ref.dtype)
+def cut_kernel(places, x_ref, layer_ref, out_ref):
+    parts, depth = out_ref.shape[:2]
+    slot_count, width = layer_ref.shape
+    across = width // LANE
+    head = depth - (SLOT_PAD // SUB) * across
     for part, i, at, size, r, c in places:
         out_ref[part, i, at : at + size, :] = x_ref[r : r + size, c : c + LANE]
-
-
-def cut_tiles(x, width, parts):
-    rows = x.shape[0]
+        if size < SUB:
+            out_ref[part, i, size:, :] = jnp.zeros((SUB - size, LANE), out_ref.dtype)
+    for at in range(0, SLOT_PAD, SUB):
+        size = min(SUB, slot_count - at)
+        for c in range(across):
+            tile = layer_ref[at : at + size, c * LANE : (c + 1) * LANE]
+            for part in range(parts):
+                out_ref[part, head + (at // SUB) * across + c, :size, :] = tile
+                if size < SUB:
+                    out_ref[part, head + (at // SUB) * across + c, size:, :] = jnp.zeros((SUB - size, LANE), tile.dtype)
+
+
+def cut_tiles(x, layer, parts):
+    rows, width = x.shape[0], layer.shape[1]
     depth, places = tile_places(rows, width, parts)
+    depth += (SLOT_PAD // SUB) * (width // LANE)
     return pl.pallas_call(
         functools.partial(cut_kernel, places),
         grid=(1,),
-        in_specs=[pl.BlockSpec((rows, width), lambda i: (0, 0))],
+        in_specs=[pl.BlockSpec((rows, width), lambda i: (0, 0)), pl.BlockSpec(layer.shape, lambda i: (0, 0))],
         out_specs=pl.BlockSpec((parts, depth, SUB, LANE), lambda i: (0, 0, 0, 0)),
         out_shape=jax.ShapeDtypeStruct((parts, depth, SUB, LANE), x.dtype),
         name="cut_tiles",
-    )(x)
+    )(x, layer)
+
+
+def gelu_parts(preact):
+    normal_cdf = 0.5 * (1.0 + lax.erf(preact * 0.7071067811865476))
+    density = jnp.exp(-0.5 * preact * preact) * 0.3989422804014327
+    return (preact * normal_cdf, normal_cdf + preact * density)
+
+
+def hidden_kernel(head, tiles_ref, gain_ref, bias_ref, weight_ref, fc1_bias_ref, normed_ref, hidden_ref, deriv_ref):
+    parts = tiles_ref.shape[0]
+    slots, width = normed_ref.shape
+    across = width // LANE
+    per_part = slots // parts
+    for part in range(parts):
+        for at in range(0, per_part, SUB):
+            for c in range(across):
+                normed_ref[part * per_part + at : part * per_part + at + SUB, c * LANE : (c + 1) * LANE] = tiles_ref[
+                    part, head + (at // SUB) * across + c
+                ]
+    values = normed_ref[...].astype(jnp.float32)
+    centered = values - jnp.mean(values, axis=1, keepdims=True)
+    row_var = jnp.mean(centered * centered, axis=1, keepdims=True)
+    normed = (centered / jnp.sqrt(row_var + 1e-05) * gain_ref[...] + bias_ref[...]).astype(jnp.bfloat16)
+    normed_ref[...] = normed
+    preact = lax.dot_general(normed, weight_ref[...], (((1,), (1,)), ((), ())), preferred_element_type=jnp.float32)
+    activated, derivative = gelu_parts(preact + fc1_bias_ref[...])
+    gap = hidden_ref.shape[1] - activated.shape[1]
+    hidden_ref[...] = jnp.zeros_like(hidden_ref)
+    hidden_ref[:, gap:] = activated.astype(jnp.bfloat16)
+    deriv_ref[...] = derivative
+
+
+def hidden_parts(tiles, head, gain, bias, weight_t, fc1_bias):
+    units, width = weight_t.shape
+    slots = tiles.shape[0] * SLOT_PAD
+    wide = -(-units // LANE) * LANE
+    return pl.pallas_call(
+        functools.partial(hidden_kernel, head),
+        out_shape=(
+            jax.ShapeDtypeStruct((slots, width), jnp.bfloat16),
+            jax.ShapeDtypeStruct((slots, wide), jnp.bfloat16),
+            jax.ShapeDtypeStruct((slots, units), jnp.float32),
+        ),
+        name="hidden_parts",
+    )(tiles, gain[None], bias[None], weight_t, fc1_bias[None])
 
 
 def grads_kernel(places, factor, tiles_ref, table_ref, normed_ref, hidden_ref, deriv_ref, weight_ref, out_ref, rows_ref, up_ref, pg_ref):
@@ -105,28 +162,54 @@
     return arrived.astype(jnp.float32).sum(axis=0).astype(jnp.bfloat16)
 
 
-def gelu_parts(preact):
-    normal_cdf = 0.5 * (1.0 + lax.erf(preact * 0.7071067811865476))
-    density = jnp.exp(-0.5 * preact * preact) * 0.3989422804014327
-    return (preact * normal_cdf, normal_cdf + preact * density)
-
-
-def slot_matrix(rank_ids, groups):
+def slot_positions(rank_ids, groups):
     columns = jnp.arange(groups, dtype=jnp.int32)
     onehot = (rank_ids[:, None] == columns[None, :]).astype(jnp.int32)
     position = jnp.cumsum(onehot, axis=0) - 1
-    own_position = jnp.sum(position * onehot, axis=1)
-    slot_ids = rank_ids * SLOT_PAD + own_position
-    targets = jnp.arange(groups * SLOT_PAD, dtype=jnp.int32)
+    return jnp.sum(position * onehot, axis=1)
+
+
+def slot_table(slot_ids, first, count):
+    targets = first + jnp.arange(count, dtype=jnp.int32)
     return (targets[:, None] == slot_ids[None, :]).astype(jnp.bfloat16)
 
 
-def normalize(layer_rows, ln_gain, ln_bias):
-    values = layer_rows.astype(jnp.float32)
-    row_mean = jnp.mean(values, axis=1, keepdims=True)
-    centered = values - row_mean
-    row_var = jnp.mean(centered * centered, axis=1, keepdims=True)
-    return (centered / jnp.sqrt(row_var + 1e-05) * ln_gain + ln_bias).astype(jnp.bfloat16)
+def plane_rounds(replicas, side):
+    rounds = []
+    for turn in range(2):
+        perms = []
+        for d in range(1, side):
+            pairs = []
+            for k in range(replicas):
+                for x in range(side):
+                    for y in range(side):
+                        along_x = (k % 2 == 0) == (turn == 0)
+                        to = ((x + d) % side, y) if along_x else (x, (y + d) % side)
+                        pairs.append(((k * side + x) * side + y, (k * side + to[0]) * side + to[1]))
+            perms.append(pairs)
+        rounds.append(perms)
+    return rounds
+
+
+def route_early(part, rank_ids, positions, replicas, groups):
+    side = int(groups**0.5)
+    rounds = plane_rounds(replicas, side)
+    me = lax.axis_index("tp")
+    dx = (rank_ids // side - me // side) % side
+    dy = (rank_ids % side - me % side) % side
+    x_first = lax.axis_index("dp") % 2 == 0
+    first, second = jnp.where(x_first, dx, dy), jnp.where(x_first, dy, dx)
+    slot_ids = (first * side + second) * SLOT_PAD + positions
+    span = side * SLOT_PAD
+    blocks = [
+        jnp.dot(slot_table(slot_ids, d * span, span), part, preferred_element_type=jnp.float32).astype(jnp.bfloat16)
+        for d in range(side)
+    ]
+    moved = [lax.ppermute(blocks[d], ("dp", "tp"), rounds[0][d - 1]) for d in range(1, side)]
+    summed = sum((b.astype(jnp.float32) for b in moved), blocks[0].astype(jnp.float32)).astype(jnp.bfloat16)
+    pieces = [summed[d * SLOT_PAD : (d + 1) * SLOT_PAD] for d in range(side)]
+    moved = [lax.ppermute(pieces[d], ("dp", "tp"), rounds[1][d - 1]) for d in range(1, side)]
+    return sum((b.astype(jnp.float32) for b in moved), pieces[0].astype(jnp.float32)).astype(jnp.bfloat16)
 
 
 def dp_groups(replicas):
@@ -154,20 +237,15 @@
     cores, near, far, pairs, close, strided = dp_groups(replicas)
     block = width // replicas
 
-    outgoing = cut_tiles(local_part, width, groups)
-    own_tiles = total(exchange(outgoing, "tp"))
-    tiles = to_all(own_tiles, "tp")
-
-    table = slot_matrix(row_rank[:, 0], groups)
-    normed = normalize(layer_input, ln_gain, ln_bias)
-    normed = jnp.pad(normed, ((0, SLOT_PAD - slot_count), (0, 0)))
-    normed_all = to_all(normed, "tp").reshape(groups * SLOT_PAD, width)
-    preact = jnp.dot(normed_all, fc1_weight, preferred_element_type=jnp.float32) + fc1_bias
-    activated, derivative = gelu_parts(preact)
-    hidden = jnp.pad(activated.astype(jnp.bfloat16), ((0, 0), (-units % LANE, 0)))
-
-    routed = jnp.dot(table, local_part[:, width:], preferred_element_type=jnp.float32).astype(jnp.bfloat16)
-    incoming = exchange(routed.reshape(groups, SLOT_PAD, routed.shape[1]), "tp")
+    arrived = exchange(cut_tiles(local_part, layer_input, groups), "tp")
+    head = arrived.shape[1] - (SLOT_PAD // SUB) * (width // LANE)
+    tiles = to_all(total(arrived[:, :head]), "tp")
+
+    rank_ids = row_rank[:, 0]
+    positions = slot_positions(rank_ids, groups)
+    table = slot_table(rank_ids * SLOT_PAD + positions, 0, groups * SLOT_PAD)
+    normed_all, hidden, derivative = hidden_parts(arrived, head, ln_gain, ln_bias, fc1_weight.T, fc1_bias)
+    placed = route_early(local_part[:, width:], rank_ids, positions, replicas, groups)[:slot_count]
 
     factor = float(replicas * row_count) ** (-0.5)
     terms = grad_terms(
@@ -177,7 +255,6 @@
     both = total(exchange(terms, "dp", pairs))
     both = total(exchange(both, "dp", close))
     both = total(exchange(both, "dp", strided))
-    placed = total(incoming)[:slot_count]
     return (placed, both[:, :units], both[:, units:])
 
 

time: 170 us -> 124 us (0.73); the launches traced: 167 us -> 123 us
  waiting for transfers between devices: 79.7 us -> 27.7 us
  Pallas kernels: 6.35 us -> 10.2 us
  matrix products: 4.05 us -> 7.01 us
  local copies, waits for them, and re-layouts: 4.22 us -> 6.32 us
    all_to_all x6 -> x4, waiting for transfers between devices: 79.7 us -> 27.7 us  [exchange(): lax.all_to_all(blocks, axis, 0, 0, tiled=True, axis_index_groups=groups)]
    all_to_all x6 -> x4, starting transfers between devices: 48.4 us -> 26.6 us  [exchange(): lax.all_to_all(blocks, axis, 0, 0, tiled=True, axis_index_groups=groups)]
    ppermute x0 -> x6, starting transfers between devices: none -> 21.1 us  [the longest x3 10.6 us: route_early(): lax.ppermute(blocks[d], ('dp', 'tp'), rounds[0][d - 1])]
    reduce_sum x5 -> x4, other arithmetic: 8.16 us -> 3.73 us  [total(): return arrived.astype(jnp.float32).sum(axis=0).astype(jnp.bfloat16)]
    pallas_call x0 -> x1, Pallas kernels: none -> 3.39 us  [hidden_parts(): pl.pallas_call(functools.partial(hidden_kernel, head), out_shape=(jax.Sha...]
    broadcast_in_dim x0 -> x3, local copies, waits for them, and re-layouts: none -> 3.16 us  [the longest x1 1.29 us: hidden_parts(): gain[None]]
    dot_general x2 -> x4, matrix products: 4.05 us -> 7.01 us  [route_early(): jnp.dot(slot_table(slot_ids, d * span, span), part, preferred_element_typ...]
    another operation x4, other arithmetic: 0.7 us -> 3.22 us
  transfers between devices with their start and end apart: 6 -> 10, of which waited for: 6 -> 3; matrix products, arithmetic and copies ran while one was open for 7% -> 19% of each run, Pallas kernels for 0% -> 6%
where the time goes in v2:
time: 124 us; the launch traced here: 123 us
  starting transfers between devices  47.7 us (38%)
  waiting for transfers between devices  27.7 us (22%)
  blocking collectives  13.2 us (11%)
  other arithmetic  10.4 us (8%)
  Pallas kernels  10.2 us (8%)
  matrix products  7.01 us (6%)
  local copies, waits for them, and re-layouts  6.32 us (5%)
    all_to_all x4, waiting for transfers between devices, exchange(): lax.all_to_all(blocks, axis, 0, 0, tiled=True, axis_index_groups=groups)  27.7 us
    all_to_all x4, starting transfers between devices, exchange(): lax.all_to_all(blocks, axis, 0, 0, tiled=True, axis_index_groups=groups)  26.6 us
    all_to_all x1, blocking collectives, exchange(): lax.all_to_all(blocks, axis, 0, 0, tiled=True, axis_index_groups=groups)  13.2 us
    ppermute x3, starting transfers between devices, route_early(): lax.ppermute(blocks[d], ('dp', 'tp'), rounds[0][d - 1])  10.6 us
    ppermute x3, starting transfers between devices, route_early(): lax.ppermute(pieces[d], ('dp', 'tp'), rounds[1][d - 1])  10.5 us
    dot_general x4, matrix products, route_early(): jnp.dot(slot_table(slot_ids, d * span, span), part, preferred_element_typ...  7.01 us
    pallas_call x1, Pallas kernels, grad_terms(): pl.pallas_call(functools.partial(grads_kernel, places, factor), out_shape...  4.49 us
    reduce_sum x4, other arithmetic, total(): return arrived.astype(jnp.float32).sum(axis=0).astype(jnp.bfloat16)  3.73 us
  transfers between devices with their start and end apart: 10, of which 3 were waited for; matrix products, arithmetic and copies ran while one was open for 19% of the time, Pallas kernels for 6%

profile of v2, /device:TPU:1, one launch (start us, length us, event | category | flops | bytes accessed | tf_op | source)
XLA Modules:
  0.0 123.3 jit_solution(11385399346926323829)
XLA Ops:
  0.7 2.4 %cut_tiles.1 = bf16[16,33,8,128]{3,2,1,0:T(8,128)(2,1)} custom-call(bf16[160,7680]{1,0:T(8,128)(2,1)} %bitcast.16, bf16[15,1280]{1,0:T(8,128)(2,1)} %layer_ref.1), custom_call_target="tpu_custom_call" | custom-call | tf_op jit(solution)/shard_map/cut_tiles/pallas_call | solution.py:54
  3.0 7.6 %all-to-all-start = ((bf16[16,33,8,128]{3,2,1,0:T(8,128)(2,1)}), bf16[16,33,8,128]{3,2,1,0:T(8,128)(2,1)S(1)}, u32[]{:S(2)}, u32[]{:S(2)}) async-start(bf16[16,33,8,128]{3,2,1,0:T(8,128)(2,1)} %cut_tiles.1), calls=%async_computation | async-start | bytes 2162688 | tf_op jit(solution)/shard_map/all_to_all | solution.py:154
  11.7 1.3 %reduce-window.6 = s32[16,2,128]{2,0,1:T(8,128)S(1)} reduce-window(s32[16,2,128]{2,0,1:T(8,128)} %copy_bitcast_fusion, s32[]{:T(128)} %constant.81.clone.1), window={size=1x1x128 pad=0_0x0_0x127_0}, to_apply=%region_0.0 | reduce-window | flops 520192 | bytes 32772 | tf_op jit(solution)/shard_map/reduce-window
  13.0 0.7 slice_reduce_fusion.1
  13.7 1.3 %reduce-window.9 = s32[16,3]{0,1:T(4,128)} reduce-window(s32[16,2]{0,1:T(2,128)} %slice_reduce_fusion.1, s32[]{:T(128)} %constant.81.clone.1), window={size=1x2 pad=0_0x2_0}, to_apply=%region_1.0 | reduce-window | flops 48 | bytes 324 | tf_op jit(solution)/shard_map/reduce-window.1
  15.8 0.7 fusion.19
  16.5 0.7 multiply_add_fusion
  17.2 2.0 %convolution_convert_fusion.2 = bf16[64,6400]{1,0:T(8,128)(2,1)} fusion(bf16[160,7680]{1,0:T(8,128)(2,1)S(1)} %bitcast.17, s32[160]{0:T(256)S(1)} %get-tuple-element.16, s32[64]{0:T(128)} %iota_add_fusion.2), kind=kOutput, calls=%fused_computation.2 | convolution fusion | flops 131491840 | bytes 2868480 | tf_op jit(solution)/shard_map/dot_general | solution.py:205
  19.3 3.2 %collective-permute-start = (bf16[64,6400]{1,0:T(8,128)(2,1)}, bf16[64,6400]{1,0:T(8,128)(2,1)}, u32[]{:S(2)}, u32[]{:S(2)}) collective-permute-start(bf16[64,6400]{1,0:T(8,128)(2,1)} %convolution_convert_fusion.2), channel_id=1, source_target_pairs={{0,4},{1,5},{2,6},{3,7},{4,8},{5,9},{6,10},{7,11},{8,12},{9,13},{1... | collective-permute-start | bytes 2457608 | tf_op jit(solution)/shard_map/ppermute | solution.py:208
  22.5 1.4 %convolution_convert_fusion.1 = bf16[64,6400]{1,0:T(8,128)(2,1)} fusion(bf16[160,7680]{1,0:T(8,128)(2,1)S(1)} %bitcast.18, s32[160]{0:T(256)S(1)} %get-tuple-element.16, s32[64]{0:T(128)S(1)} %iota_add_fusion.1), kind=kOutput, calls=%fused_computation.1 | convolution fusion | flops 131491840 | bytes 2868736 | tf_op jit(solution)/shard_map/dot_general | solution.py:205
  23.9 4.3 %collective-permute-start.1 = (bf16[64,6400]{1,0:T(8,128)(2,1)}, bf16[64,6400]{1,0:T(8,128)(2,1)}, u32[]{:S(2)}, u32[]{:S(2)}) collective-permute-start(bf16[64,6400]{1,0:T(8,128)(2,1)} %convolution_convert_fusion.1), channel_id=1, source_target_pairs={{0,8},{1,9},{2,10},{3,11},{4,12},{5,13},{6,14},{7,15},{8,0},{9,1},... | collective-permute-start | bytes 2457608 | tf_op jit(solution)/shard_map/ppermute | solution.py:208
  28.2 1.4 %convolution_convert_fusion = bf16[64,6400]{1,0:T(8,128)(2,1)} fusion(bf16[160,7680]{1,0:T(8,128)(2,1)S(1)} %bitcast.19, s32[160]{0:T(256)S(1)} %get-tuple-element.16, s32[64]{0:T(128)S(1)} %iota_add_fusion), kind=kOutput, calls=%fused_computation | convolution fusion | flops 131491840 | bytes 2868736 | tf_op jit(solution)/shard_map/dot_general | solution.py:205
  29.6 3.1 %collective-permute-start.2 = (bf16[64,6400]{1,0:T(8,128)(2,1)}, bf16[64,6400]{1,0:T(8,128)(2,1)}, u32[]{:S(2)}, u32[]{:S(2)}) collective-permute-start(bf16[64,6400]{1,0:T(8,128)(2,1)} %convolution_convert_fusion), channel_id=1, source_target_pairs={{0,12},{1,13},{2,14},{3,15},{4,0},{5,1},{6,2},{7,3},{8,4},{9,5},{1... | collective-permute-start | bytes 2457608 | tf_op jit(solution)/shard_map/ppermute | solution.py:208
  32.8 1.0 broadcast_in_dim.8
  33.7 4.2 %all-to-all-start.1 = ((bf16[16,13,8,128]{3,2,1,0:T(8,128)(2,1)}), bf16[16,13,8,128]{3,2,1,0:T(8,128)(2,1)}, u32[]{:S(2)}, u32[]{:S(2)}) async-start(bf16[16,13,8,128]{3,2,1,0:T(8,128)(2,1)} %broadcast_in_dim.8), calls=%async_computation.1 | async-start | bytes 851968 | tf_op jit(solution)/shard_map/all_to_all | solution.py:154
  38.6 1.3 %broadcast_in_dim.9.gain_ref = f32[1,1280]{1,0:T(1,128)} reshape(f32[1280]{0:T(1024)} %param.10) | data formatting | bytes 10240 | tf_op jit(solution)/shard_map/broadcast_in_dim | solution.py:106
  39.9 1.3 %broadcast_in_dim.11.fc1_bias_ref = f32[1,320]{1,0:T(1,128)} reshape(f32[320]{0:T(512)} %param.13) | data formatting | bytes 2560 | tf_op jit(solution)/shard_map/broadcast_in_dim | solution.py:106
  41.8 3.4 %hidden_parts.1 = (bf16[256,1280]{1,0:T(8,128)(2,1)}, bf16[256,384]{1,0:T(8,128)(2,1)}, f32[256,320]{1,0:T(8,128)}) custom-call(bf16[16,33,8,128]{3,2,1,0:T(8,128)(2,1)} %copy-done.1, f32[1,1280]{1,0:T(1,128)} %broadcast_in_dim.9.gain_ref, f32[1,1280]{1,0:T(1,128)} %broadcast_in_dim.10.bias_ref, bf16[320,1280]{1,0:T(8,128)(2,1)} %bitcast.21, ...), custom_call_target="tpu_custom_call" | custom-call | tf_op jit(solution)/shard_map/hidden_parts/pallas_call | solution.py:98
  45.2 6.9 %all-to-all-done.1.tiles_ref = bf16[16,13,8,128]{3,2,1,0:T(8,128)(2,1)} async-done(((bf16[16,13,8,128]{3,2,1,0:T(8,128)(2,1)}), bf16[16,13,8,128]{3,2,1,0:T(8,128)(2,1)}, u32[]{:S(2)}, u32[]{:S(2)}) %all-to-all-start.1) | async-done | bytes 426016 | tf_op jit(solution)/shard_map/all_to_all | solution.py:154
  52.1 4.5 %grad_terms.1 = bf16[2,4,4,40,640]{4,3,2,1,0:T(8,128)(2,1)} custom-call(bf16[16,13,8,128]{3,2,1,0:T(8,128)(2,1)} %all-to-all-done.1.tiles_ref, bf16[256,160]{1,0:T(8,128)(2,1)} %fusion.7.table_ref, bf16[256,1280]{1,0:T(8,128)(2,1)} %get-tuple-element.6.normed_ref, bf16[256,384]{1,0:T(8,128)(2,1)} %get-tuple-element.7.hidden_ref, ...), custom_call_target="tpu_custom_call" | custom-call | tf_op jit(solution)/shard_map/grad_terms/pallas_call | solution.py:141
  56.6 13.2 %all_to_all.25 = bf16[2,4,4,40,640]{4,3,2,1,0:T(8,128)(2,1)} all-to-all(bf16[2,4,4,40,640]{4,3,2,1,0:T(8,128)(2,1)} %grad_terms.1), channel_id=1, replica_groups={{0,16},{32,48},{64,80},{96,112},{128,144},{160,176},{192,208},{224,240}..., dimensions={0} | all-to-all | bytes 3276800 | tf_op jit(solution)/shard_map/all_to_all | solution.py:154
  69.8 2.8 %reduce_sum.59 = bf16[4,4,40,640]{3,2,1,0:T(8,128)(2,1)} reduce(bf16[2,4,4,40,640]{4,3,2,1,0:T(8,128)(2,1)} %all_to_all.25, bf16[]{:T(256)} %constant.93.clone.1), dimensions={0}, to_apply=%region_4.5 | reduce | flops 409600 | bytes 2457602 | tf_op jit(solution)/shard_map/reduce_sum | solution.py:162
  72.6 9.0 %all-to-all-start.3 = ((bf16[4,4,40,640]{3,2,1,0:T(8,128)(2,1)}), bf16[4,4,40,640]{3,2,1,0:T(8,128)(2,1)S(1)}, u32[]{:S(2)}, u32[]{:S(2)}) async-start(bf16[4,4,40,640]{3,2,1,0:T(8,128)(2,1)} %reduce_sum.59), calls=%async_computation.3 | async-start | bytes 1638400 | tf_op jit(solution)/shard_map/all_to_all | solution.py:154
  81.6 2.2 %add_convert_fusion = bf16[64,6400]{1,0:T(8,128)(2,1)S(1)} fusion(bf16[64,6400]{1,0:T(8,128)(2,1)} %collective-permute-done.2, bf16[64,6400]{1,0:T(8,128)(2,1)} %collective-permute-done.1, bf16[64,6400]{1,0:T(8,128)(2,1)} %collective-permute-done, bf16[160,7680]{1,0:T(8,128)(2,1)S(1)} %bitcast.20, s32[160]{0:T(256)S(1)} %get-tuple-element.16), kind=kOutput, calls=%fused_computation.5 | convolution fusion | flops 134768640 | bytes 5325824 | tf_op jit(solution)/shard_map/dot_general | solution.py:205
  83.9 3.9 %collective-permute-start.3 = (bf16[16,6400]{1,0:T(8,128)(2,1)S(1)}, bf16[16,6400]{1,0:T(8,128)(2,1)S(1)}, u32[]{:S(2)}, u32[]{:S(2)}) collective-permute-start(bf16[16,6400]{1,0:T(8,128)(2,1)S(1)} %get-tuple-element.12), channel_id=1, source_target_pairs={{0,1},{1,2},{2,3},{3,0},{4,5},{5,6},{6,7},{7,4},{8,9},{9,10},{10,1... | collective-permute-start | bytes 614408 | tf_op jit(solution)/shard_map/ppermute | solution.py:211
  87.8 3.4 %collective-permute-start.4 = (bf16[16,6400]{1,0:T(8,128)(2,1)S(1)}, bf16[16,6400]{1,0:T(8,128)(2,1)S(1)}, u32[]{:S(2)}, u32[]{:S(2)}) collective-permute-start(bf16[16,6400]{1,0:T(8,128)(2,1)S(1)} %get-tuple-element.11), channel_id=1, source_target_pairs={{0,2},{1,3},{2,0},{3,1},{4,6},{5,7},{6,4},{7,5},{8,10},{9,11},{10,... | collective-permute-start | bytes 614408 | tf_op jit(solution)/shard_map/ppermute | solution.py:211
  91.3 3.1 %collective-permute-start.5 = (bf16[16,6400]{1,0:T(8,128)(2,1)S(1)}, bf16[16,6400]{1,0:T(8,128)(2,1)S(1)}, u32[]{:S(2)}, u32[]{:S(2)}) collective-permute-start(bf16[16,6400]{1,0:T(8,128)(2,1)S(1)} %get-tuple-element.10), channel_id=1, source_target_pairs={{0,3},{1,0},{2,1},{3,2},{4,7},{5,4},{6,5},{7,6},{8,11},{9,8},{10,9... | collective-permute-start | bytes 614408 | tf_op jit(solution)/shard_map/ppermute | solution.py:211
  94.4 5.1 %all-to-all-done.3 = bf16[4,4,40,640]{3,2,1,0:T(8,128)(2,1)S(1)} async-done(((bf16[4,4,40,640]{3,2,1,0:T(8,128)(2,1)}), bf16[4,4,40,640]{3,2,1,0:T(8,128)(2,1)S(1)}, u32[]{:S(2)}, u32[]{:S(2)}) %all-to-all-start.3) | async-done | bytes 819232 | tf_op jit(solution)/shard_map/all_to_all | solution.py:154
  99.5 0.8 reduce_sum.60
  100.3 5.8 %all-to-all-start.4 = ((bf16[4,40,640]{2,1,0:T(8,128)(2,1)}), bf16[4,40,640]{2,1,0:T(8,128)(2,1)S(1)}, u32[]{:S(2)}, u32[]{:S(2)}) async-start(bf16[4,40,640]{2,1,0:T(8,128)(2,1)} %reduce_sum.60), calls=%async_computation.4 | async-start | bytes 409600 | tf_op jit(solution)/shard_map/all_to_all | solution.py:154
  106.2 0.8 add_convert_fusion.1
  106.9 15.7 %all-to-all-done.4 = bf16[4,40,640]{2,1,0:T(8,128)(2,1)S(1)} async-done(((bf16[4,40,640]{2,1,0:T(8,128)(2,1)}), bf16[4,40,640]{2,1,0:T(8,128)(2,1)S(1)}, u32[]{:S(2)}, u32[]{:S(2)}) %all-to-all-start.4) | async-done | bytes 204832 | tf_op jit(solution)/shard_map/all_to_all | solution.py:154
  (28 shorter events, 4.1 us)
Async XLA Ops:
  0.6 10.5 %copy-start.2 = (s32[160,1]{0,1:T(1,128)S(1)}, s32[160,1]{0,1:T(1,128)}, u32[]{:S(2)}) copy-start(s32[160,1]{0,1:T(1,128)} %param.15) | copy-start | bytes 1924
  0.6 16.6 %copy-start = (bf16[1,160,7680]{2,1,0:T(8,128)(2,1)S(1)}, bf16[1,160,7680]{2,1,0:T(8,128)(2,1)}, u32[]{:S(2)}) copy-start(bf16[1,160,7680]{2,1,0:T(8,128)(2,1)} %param.8) | copy-start | bytes 7372804
  3.0 29.7 %all-to-all-start = ((bf16[16,33,8,128]{3,2,1,0:T(8,128)(2,1)}), bf16[16,33,8,128]{3,2,1,0:T(8,128)(2,1)S(1)}, u32[]{:S(2)}, u32[]{:S(2)}) async-start(bf16[16,33,8,128]{3,2,1,0:T(8,128)(2,1)} %cut_tiles.1), calls=%async_computation | async-start | bytes 2162688 | tf_op jit(solution)/shard_map/all_to_all | solution.py:154
  19.3 62.4 %collective-permute-start = (bf16[64,6400]{1,0:T(8,128)(2,1)}, bf16[64,6400]{1,0:T(8,128)(2,1)}, u32[]{:S(2)}, u32[]{:S(2)}) collective-permute-start(bf16[64,6400]{1,0:T(8,128)(2,1)} %convolution_convert_fusion.2), channel_id=1, source_target_pairs={{0,4},{1,5},{2,6},{3,7},{4,8},{5,9},{6,10},{7,11},{8,12},{9,13},{1... | collective-permute-start | bytes 2457608 | tf_op jit(solution)/shard_map/ppermute | solution.py:208
  23.9 57.7 %collective-permute-start.1 = (bf16[64,6400]{1,0:T(8,128)(2,1)}, bf16[64,6400]{1,0:T(8,128)(2,1)}, u32[]{:S(2)}, u32[]{:S(2)}) collective-permute-start(bf16[64,6400]{1,0:T(8,128)(2,1)} %convolution_convert_fusion.1), channel_id=1, source_target_pairs={{0,8},{1,9},{2,10},{3,11},{4,12},{5,13},{6,14},{7,15},{8,0},{9,1},... | collective-permute-start | bytes 2457608 | tf_op jit(solution)/shard_map/ppermute | solution.py:208
  28.2 9.7 %copy-start.3 = (f32[1280]{0:T(1024)S(1)}, f32[1280]{0:T(1024)}, u32[]{:S(2)}) copy-start(f32[1280]{0:T(1024)} %param.11) | copy-start | bytes 15364
  29.6 52.0 %collective-permute-start.2 = (bf16[64,6400]{1,0:T(8,128)(2,1)}, bf16[64,6400]{1,0:T(8,128)(2,1)}, u32[]{:S(2)}, u32[]{:S(2)}) collective-permute-start(bf16[64,6400]{1,0:T(8,128)(2,1)} %convolution_convert_fusion), channel_id=1, source_target_pairs={{0,12},{1,13},{2,14},{3,15},{4,0},{5,1},{6,2},{7,3},{8,4},{9,5},{1... | collective-permute-start | bytes 2457608 | tf_op jit(solution)/shard_map/ppermute | solution.py:208
  32.7 9.1 %copy-start.1 = (bf16[16,33,8,128]{3,2,1,0:T(8,128)(2,1)}, bf16[16,33,8,128]{3,2,1,0:T(8,128)(2,1)S(1)}, u32[]{:S(2)}) copy-start(bf16[16,33,8,128]{3,2,1,0:T(8,128)(2,1)S(1)} %all-to-all-done.tiles_ref) | copy-start | bytes 3244036
  33.7 18.4 %all-to-all-start.1 = ((bf16[16,13,8,128]{3,2,1,0:T(8,128)(2,1)}), bf16[16,13,8,128]{3,2,1,0:T(8,128)(2,1)}, u32[]{:S(2)}, u32[]{:S(2)}) async-start(bf16[16,13,8,128]{3,2,1,0:T(8,128)(2,1)} %broadcast_in_dim.8), calls=%async_computation.1 | async-start | bytes 851968 | tf_op jit(solution)/shard_map/all_to_all | solution.py:154
  72.6 26.9 %all-to-all-start.3 = ((bf16[4,4,40,640]{3,2,1,0:T(8,128)(2,1)}), bf16[4,4,40,640]{3,2,1,0:T(8,128)(2,1)S(1)}, u32[]{:S(2)}, u32[]{:S(2)}) async-start(bf16[4,4,40,640]{3,2,1,0:T(8,128)(2,1)} %reduce_sum.59), calls=%async_computation.3 | async-start | bytes 1638400 | tf_op jit(solution)/shard_map/all_to_all | solution.py:154
  83.9 22.2 %collective-permute-start.3 = (bf16[16,6400]{1,0:T(8,128)(2,1)S(1)}, bf16[16,6400]{1,0:T(8,128)(2,1)S(1)}, u32[]{:S(2)}, u32[]{:S(2)}) collective-permute-start(bf16[16,6400]{1,0:T(8,128)(2,1)S(1)} %get-tuple-element.12), channel_id=1, source_target_pairs={{0,1},{1,2},{2,3},{3,0},{4,5},{5,6},{6,7},{7,4},{8,9},{9,10},{10,1... | collective-permute-start | bytes 614408 | tf_op jit(solution)/shard_map/ppermute | solution.py:211
  87.8 18.3 %collective-permute-start.4 = (bf16[16,6400]{1,0:T(8,128)(2,1)S(1)}, bf16[16,6400]{1,0:T(8,128)(2,1)S(1)}, u32[]{:S(2)}, u32[]{:S(2)}) collective-permute-start(bf16[16,6400]{1,0:T(8,128)(2,1)S(1)} %get-tuple-element.11), channel_id=1, source_target_pairs={{0,2},{1,3},{2,0},{3,1},{4,6},{5,7},{6,4},{7,5},{8,10},{9,11},{10,... | collective-permute-start | bytes 614408 | tf_op jit(solution)/shard_map/ppermute | solution.py:211
  91.3 14.9 %collective-permute-start.5 = (bf16[16,6400]{1,0:T(8,128)(2,1)S(1)}, bf16[16,6400]{1,0:T(8,128)(2,1)S(1)}, u32[]{:S(2)}, u32[]{:S(2)}) collective-permute-start(bf16[16,6400]{1,0:T(8,128)(2,1)S(1)} %get-tuple-element.10), channel_id=1, source_target_pairs={{0,3},{1,0},{2,1},{3,2},{4,7},{5,4},{6,5},{7,6},{8,11},{9,8},{10,9... | collective-permute-start | bytes 614408 | tf_op jit(solution)/shard_map/ppermute | solution.py:211
  100.3 22.3 %all-to-all-start.4 = ((bf16[4,40,640]{2,1,0:T(8,128)(2,1)}), bf16[4,40,640]{2,1,0:T(8,128)(2,1)S(1)}, u32[]{:S(2)}, u32[]{:S(2)}) async-start(bf16[4,40,640]{2,1,0:T(8,128)(2,1)} %reduce_sum.60), calls=%async_computation.4 | async-start | bytes 409600 | tf_op jit(solution)/shard_map/all_to_all | solution.py:154
